TPU v7x, 32 devices: a whole 2x2x4 slice. The times are simulated.
32 devices in a mesh: north: 8 (over z, x), deep: 4 (over y, core).
Axes of the slice: x: 2, y: 2, z: 4, core: 2. Of those that a mesh axis runs over, the one named last changes fastest.
Arguments:
- source: float32 [128, 128, 2048], P(None, 'north', 'deep'), may hold values from -6 to 6
- symbol_x: float32 [128], replicated, may hold values from 0.3 to 3
- symbol_y: float32 [128], replicated, may hold values from 0.3 to 3
- symbol_z: float32 [2048], replicated, may hold values from 0.3 to 3
Outputs:
- coefficients: float32 [64, 64, 1024], P('north', 'deep')
All inputs are finite; a program needn't handle non-finite values.
Results may differ from a plain program's by a relative error of at most 0.000071.
Values sent between devices are 32-bit elements; how exact they have to be, the bound alone decides.
A program may use at most 128 MiB of HBM per device.

v0:
```python
import jax
import jax.numpy as jnp
from jax import lax
from jax.sharding import PartitionSpec as P


def basis_table(count):
    rank = jnp.arange(count)
    angle = (
        jnp.pi
        / (count + 1)
        * ((rank[:, None] + 1) * (rank[None, :] + 1) % (2 * count + 2)).astype(jnp.float32)
    )
    return jnp.sin(angle) * (2.0 / (count + 1)) ** 0.5


def along_dim(values, dim):
    moved = jnp.tensordot(
        values, basis_table(values.shape[dim]), axes=([dim], [0]), precision=lax.Precision.HIGHEST
    )
    return jnp.moveaxis(moved, -1, dim)


def on_device(source, symbol_x, symbol_y, symbol_z):
    part_values = source
    part_values = along_dim(part_values, 0)
    part_values = lax.slice_in_dim(part_values, 0, part_values.shape[0] // 2, axis=0)
    part_values = lax.all_to_all(part_values, "north", split_axis=0, concat_axis=1, tiled=True)
    part_values = along_dim(part_values, 1)
    pencil_values = lax.slice_in_dim(part_values, 0, part_values.shape[1] // 2, axis=1)
    pencil_values = lax.all_to_all(pencil_values, "deep", split_axis=1, concat_axis=2, tiled=True)
    pencil_values = along_dim(pencil_values, 2)
    pencil_values = lax.slice_in_dim(pencil_values, 0, pencil_values.shape[2] // 2, axis=2)
    share_x = pencil_values.shape[0]
    part_x = lax.dynamic_slice_in_dim(symbol_x, lax.axis_index("north") * share_x, share_x)
    share_y = pencil_values.shape[1]
    part_y = lax.dynamic_slice_in_dim(symbol_y, lax.axis_index("deep") * share_y, share_y)
    symbol = (
        part_x[:, None, None]
        + part_y[None, :, None]
        + symbol_z[: pencil_values.shape[2]][None, None, :]
    )
    pencil_values = pencil_values * lax.rsqrt(symbol)
    return pencil_values


def solution(mesh):
    in_specs = (P(None, "north", "deep"), P(), P(), P())
    out_specs = P("north", "deep", None)
    return jax.shard_map(
        on_device, mesh=mesh, in_specs=in_specs, out_specs=out_specs, check_vma=False
    )
```

profile of v0, /device:TPU:0, one launch (start us, length us, event | category | flops | bytes accessed | tf_op | source)
XLA Modules:
  0.0 149.1 jit_solution(16678220194207487716)
XLA Ops:
  0.0 0.3 fusion.19
  0.3 7.2 %fusion.10 = f32[64,16,512]{2,0,1:T(8,128)S(1)} fusion(f32[128,16,512]{2,1,0:T(8,128)} %param.4, f32[128,128,1]{0,1,2:T(8,128)S(1)} %fusion.19), kind=kOutput, calls=%fused_computation.12 | convolution fusion | flops 805306368 | bytes 6324224 | tf_op jit(solution)/shard_map/dot_general | solution.py:18
  7.5 2.6 %copy.9 = f32[64,16,512]{2,1,0:T(8,128)} copy(f32[64,16,512]{2,0,1:T(8,128)S(1)} %fusion.10) | data formatting | bytes 4194304 | tf_op jit(solution)/shard_map/slice | solution.py:27
  10.1 7.3 %all-to-all-start = ((f32[64,16,512]{2,1,0:T(8,128)}), f32[64,16,512]{2,1,0:T(8,128)S(1)}, u32[]{:S(2)}, u32[]{:S(2)}) async-start(f32[64,16,512]{2,1,0:T(8,128)} %copy.9), calls=%async_computation | async-start | bytes 4194304 | tf_op jit(solution)/shard_map/all_to_all | solution.py:28
  17.4 48.2 %all-to-all-done = f32[64,16,512]{2,1,0:T(8,128)S(1)} async-done(((f32[64,16,512]{2,1,0:T(8,128)}), f32[64,16,512]{2,1,0:T(8,128)S(1)}, u32[]{:S(2)}, u32[]{:S(2)}) %all-to-all-start) | async-done | bytes 2097184 | tf_op jit(solution)/shard_map/all_to_all | solution.py:28
  65.6 0.2 copy.10
  65.8 2.4 %convolution_bitcast_fusion = f32[8,128,512]{2,1,0:T(8,128)S(1)} fusion(f32[8,128,512]{2,1,0:T(8,128)S(1)} %bitcast.17, s32[128]{0:T(128)S(1)} %iota_add_fusion.1), kind=kOutput, calls=%fused_computation.14 | convolution fusion | flops 805470208 | bytes 4194816 | tf_op jit(solution)/shard_map/dot_general | solution.py:18
  68.2 0.1 slice.19
  68.3 1.6 %copy.11 = f32[8,64,512]{2,0,1:T(8,128)} copy(f32[8,64,512]{2,1,0:T(8,128)S(1)} %slice.19) | data formatting | bytes 2097152 | tf_op jit(solution)/shard_map/slice | solution.py:30
  69.9 3.7 %all-to-all-start.1 = ((f32[8,64,512]{2,0,1:T(8,128)}), f32[8,64,512]{2,0,1:T(8,128)S(1)}, u32[]{:S(2)}, u32[]{:S(2)}) async-start(f32[8,64,512]{2,0,1:T(8,128)} %copy.11), calls=%async_computation.1 | async-start | bytes 2097152 | tf_op jit(solution)/shard_map/all_to_all | solution.py:31
  73.6 0.0 copy-start
  73.6 0.0 copy-start.1
  73.6 0.0 slice-start
  73.7 65.9 %fusion.4 = f32[2048,2048,1]{1,0,2:T(8,128)} fusion(s32[2048]{0:T(1024)S(1)} %iota_add_fusion), kind=kLoop, calls=%fused_computation.5 | loop fusion | flops 41943040 | bytes 16785408 | tf_op jit(solution)/shard_map/mul | solution.py:14
  139.5 0.0 copy-done
  139.5 0.1 dynamic_slice.7
  139.6 0.0 copy-done.1
  139.6 0.1 dynamic_slice.6
  139.7 0.1 broadcast_add_fusion
  139.8 0.0 all-to-all-done.1
  139.8 0.7 copy.16
  140.4 0.7 all_to_all.33
  141.2 0.0 slice-done
  141.2 7.9 %fusion.12 = f32[8,16,1024]{2,1,0:T(8,128)} fusion(f32[8,16,2048]{2,1,0:T(8,128)S(1)} %all_to_all.33, f32[2048,2048,1]{1,0,2:T(8,128)} %fusion.4, f32[1024]{0:T(1024)S(1)} %slice-done, f32[8,16]{1,0:T(8,128)S(1)} %broadcast_add_fusion), kind=kOutput, calls=%fused_computation.15 | convolution fusion | flops 3221487616 | bytes 9966080 | tf_op jit(solution)/shard_map/dot_general | solution.py:18
  (2 shorter events, 0.0 us)
Async XLA Ops:
  10.1 55.5 %all-to-all-start = ((f32[64,16,512]{2,1,0:T(8,128)}), f32[64,16,512]{2,1,0:T(8,128)S(1)}, u32[]{:S(2)}, u32[]{:S(2)}) async-start(f32[64,16,512]{2,1,0:T(8,128)} %copy.9), calls=%async_computation | async-start | bytes 4194304 | tf_op jit(solution)/shard_map/all_to_all | solution.py:28
  69.9 69.9 %all-to-all-start.1 = ((f32[8,64,512]{2,0,1:T(8,128)}), f32[8,64,512]{2,0,1:T(8,128)S(1)}, u32[]{:S(2)}, u32[]{:S(2)}) async-start(f32[8,64,512]{2,0,1:T(8,128)} %copy.11), calls=%async_computation.1 | async-start | bytes 2097152 | tf_op jit(solution)/shard_map/all_to_all | solution.py:31
  73.6 65.9 %copy-start = (f32[128]{0:T(128)S(1)}, f32[128]{0:T(128)}, u32[]{:S(2)}) copy-start(f32[128]{0:T(128)} %param.6) | copy-start | bytes 1540
  73.6 66.0 %copy-start.1 = (f32[128]{0:T(128)S(1)}, f32[128]{0:T(128)}, u32[]{:S(2)}) copy-start(f32[128]{0:T(128)} %param.5) | copy-start | bytes 1540
  73.6 67.5 %slice-start = ((f32[2048]{0:T(1024)}), f32[1024]{0:T(1024)S(1)}, s32[]{:S(2)}) async-start(f32[2048]{0:T(1024)} %param.7), calls=%async_computation.2 | async-start | bytes 8192 | tf_op jit(solution)/shard_map/slice | solution.py:41
where the time goes:
time: 149 us
  other arithmetic  66.3 us (44%)
  waiting for transfers between devices  48.2 us (32%)
  matrix products  17.5 us (12%)
  starting transfers between devices  11 us (7%)
  local copies, waits for them, and re-layouts  5.99 us (4%)
    mul x2, other arithmetic, basis_table(): return jnp.sin(angle) * (2.0 / (count + 1)) ** 0.5  66.2 us
    all_to_all x1, waiting for transfers between devices, on_device(): lax.all_to_all(part_values, 'north', split_axis=0, concat_axis=1, tiled=T...  48.2 us
    dot_general x3, matrix products, along_dim(): jnp.tensordot(values, basis_table(values.shape[dim]), axes=([dim], [0]),...  17.5 us
    all_to_all x1, starting transfers between devices, on_device(): lax.all_to_all(part_values, 'north', split_axis=0, concat_axis=1, tiled=T...  7.28 us
    all_to_all x1, starting transfers between devices, on_device(): lax.all_to_all(pencil_values, 'deep', split_axis=1, concat_axis=2, tiled=...  3.7 us
  transfers between devices with their start and end apart: 2, of which 1 were waited for; matrix products, arithmetic and copies ran while one was open for 44% of the time, Pallas kernels for 0%

commit v1 on v0

v1 whole, which is shorter than its diff:
```python
import jax
import jax.numpy as jnp
import numpy as np
from jax import lax
from jax.sharding import PartitionSpec as P

HIGH = lax.Precision.HIGH


def small_table(rows, modes, count):
    rank = np.outer(rows, modes) % (2 * count + 2)
    return np.pi / (count + 1) * rank


def kept_table(count):
    angle = small_table(np.arange(1, count + 1), np.arange(1, count // 2 + 1), count)
    return jnp.asarray((np.sin(angle) * (2.0 / (count + 1)) ** 0.5).astype(np.float32))


def long_table(count, fine=32):
    modes = np.arange(1, count // 2 + 1)
    gain = (2.0 / (count + 1)) ** 0.5
    coarse = small_table(np.arange(0, count, fine), modes, count)
    step = small_table(np.arange(1, fine + 1), modes, count)
    f32 = lambda v: jnp.asarray(v.astype(np.float32))
    sin_a, cos_a = f32(np.sin(coarse) * gain), f32(np.cos(coarse) * gain)
    sin_b, cos_b = f32(np.sin(step)), f32(np.cos(step))
    table = sin_a[:, None, :] * cos_b[None] + cos_a[:, None, :] * sin_b[None]
    return table.reshape(count, count // 2)


def on_device(source, symbol_x, symbol_y, symbol_z):
    north, deep = lax.axis_size("north"), lax.axis_size("deep")
    nx, ny_part, nz_part = source.shape
    each = nx // 2 // north // deep
    v = jnp.einsum("xk,xyz->kyz", kept_table(nx), source, precision=HIGH)
    v = v.reshape(north, deep, each, ny_part, nz_part)
    v = lax.all_to_all(v, "deep", split_axis=1, concat_axis=4, tiled=True)
    v = v.reshape(north, each, ny_part, nz_part * deep)
    v = jnp.einsum("neyz,zk->neyk", v, long_table(nz_part * deep), precision=HIGH)
    v = lax.all_to_all(v, "north", split_axis=0, concat_axis=2, tiled=True)
    v = v.reshape(each, ny_part * north, v.shape[-1])
    v = jnp.einsum("eyz,yk->ekz", v, kept_table(ny_part * north), precision=HIGH)
    v = lax.all_to_all(v, "deep", split_axis=1, concat_axis=0, tiled=True)
    part_x = lax.dynamic_slice_in_dim(symbol_x, lax.axis_index("north") * v.shape[0], v.shape[0])
    part_y = lax.dynamic_slice_in_dim(symbol_y, lax.axis_index("deep") * v.shape[1], v.shape[1])
    symbol = part_x[:, None, None] + part_y[None, :, None] + symbol_z[: v.shape[2]][None, None, :]
    return v * lax.rsqrt(symbol)


def solution(mesh):
    in_specs = (P(None, "north", "deep"), P(), P(), P())
    out_specs = P("north", "deep", None)
    return jax.shard_map(
        on_device, mesh=mesh, in_specs=in_specs, out_specs=out_specs, check_vma=False
    )
```

time: 149 us -> 102 us (0.68)
  other arithmetic: 66.3 us -> 5.65 us
  blocking collectives: 0 us -> 32 us
  waiting for transfers between devices: 48.2 us -> 29.6 us
  local copies, waits for them, and re-layouts: 5.99 us -> 13.6 us
  matrix products: 17.5 us -> 12.5 us
  starting transfers between devices: 11 us -> 7.74 us
    mul x2 -> x1, other arithmetic: 66.2 us -> 0.94 us  [on_device(): return v * lax.rsqrt(symbol)]
    all_to_all x0 -> x1, blocking collectives: none -> 32 us  [on_device(): v = lax.all_to_all(v, 'north', split_axis=0, concat_axis=2, tiled=True)]
    all_to_all x2, waiting for transfers between devices: 48.2 us -> 29.6 us  [the longest x1 21 us: on_device(): v = lax.all_to_all(v, 'deep', split_axis=1, concat_axis=4, tiled=True)]
    reshape x0 -> x3, local copies, waits for them, and re-layouts: none -> 9.23 us  [the longest x2 6.54 us: on_device(): v = v.reshape(north, deep, each, ny_part, nz_part)]
    dot_general x3, matrix products: 17.5 us -> 12.5 us  [the longest x1 6.47 us: on_device(): jnp.einsum('neyz,zk->neyk', v, long_table(nz_part * deep), precision=HIGH)]
    add x2 -> x1, other arithmetic: 0.01 us -> 4.63 us  [long_table(): table = sin_a[:, None, :] * cos_b[None] + cos_a[:, None, :] * sin_b[None]]
    slice x5 -> x2, local copies, waits for them, and re-layouts: 4.26 us -> 0.01 us  [on_device(): symbol_z[:v.shape[2]][None, None, :]]
    all_to_all x2, starting transfers between devices: 11 us -> 7.74 us  [the longest x1 4.27 us: on_device(): v = lax.all_to_all(v, 'deep', split_axis=1, concat_axis=4, tiled=True)]
  transfers between devices with their start and end apart: 2 -> 2, of which waited for: 1 -> 2; matrix products, arithmetic and copies ran while one was open for 44% -> 5% of each run, Pallas kernels for 0% -> 0%
where the time goes in v1:
time: 102 us; the launch traced here: 101 us
  blocking collectives  32 us (31%)
  waiting for transfers between devices  29.6 us (29%)
  local copies, waits for them, and re-layouts  13.6 us (13%)
  matrix products  12.5 us (12%)
  starting transfers between devices  7.74 us (8%)
  other arithmetic  5.65 us (6%)
    all_to_all x1, blocking collectives, on_device(): v = lax.all_to_all(v, 'north', split_axis=0, concat_axis=2, tiled=True)  32 us
    all_to_all x1, waiting for transfers between devices, on_device(): v = lax.all_to_all(v, 'deep', split_axis=1, concat_axis=4, tiled=True)  21 us
    all_to_all x1, waiting for transfers between devices, on_device(): v = lax.all_to_all(v, 'deep', split_axis=1, concat_axis=0, tiled=True)  8.54 us
    reshape x2, local copies, waits for them, and re-layouts, on_device(): v = v.reshape(north, deep, each, ny_part, nz_part)  6.54 us
    dot_general x1, matrix products, on_device(): jnp.einsum('neyz,zk->neyk', v, long_table(nz_part * deep), precision=HIGH)  6.47 us
    dot_general x1, matrix products, on_device(): v = jnp.einsum('xk,xyz->kyz', kept_table(nx), source, precision=HIGH)  5.65 us
    add x1, other arithmetic, long_table(): table = sin_a[:, None, :] * cos_b[None] + cos_a[:, None, :] * sin_b[None]  4.63 us
    all_to_all x1, starting transfers between devices, on_device(): v = lax.all_to_all(v, 'deep', split_axis=1, concat_axis=4, tiled=True)  4.27 us
  transfers between devices with their start and end apart: 2, of which 2 were waited for; matrix products, arithmetic and copies ran while one was open for 5% of the time, Pallas kernels for 0%

profile of v1, /device:TPU:0, one launch (start us, length us, event | category | flops | bytes accessed | tf_op | source)
XLA Modules:
  0.0 101.3 jit_solution(16082460734918682209)
XLA Ops:
  0.0 5.6 %fusion = f32[64,16,512]{2,0,1:T(8,128)S(1)} fusion(f32[128,64,1]{0,1,2:T(8,128)} %constant.32, f32[128,16,512]{2,1,0:T(8,128)} %param.10), kind=kOutput, calls=%fused_computation.1 | convolution fusion | flops 402653184 | bytes 6324224 | tf_op jit(solution)/shard_map/xk,xyz->kyz/dot_general | solution.py:36
  5.7 2.3 %reshape.69 = f32[8,4,2,16,512]{4,2,1,0,3:T(2,128)} reshape(f32[64,16,512]{2,0,1:T(8,128)S(1)} %fusion) | data formatting | bytes 4194304 | tf_op jit(solution)/shard_map/reshape | solution.py:37
  7.9 0.0 copy-start
  7.9 0.0 copy-start.1
  7.9 0.0 copy-start.2
  7.9 0.0 copy-start.3
  7.9 4.3 %copy.19 = f32[8,4,2,16,512]{4,2,0,3,1:T(2,128)} copy(f32[8,4,2,16,512]{4,2,1,0,3:T(2,128)} %reshape.69) | data formatting | bytes 4194304 | tf_op jit(solution)/shard_map/reshape | solution.py:37
  12.2 4.3 %all-to-all-start = ((f32[8,4,2,16,512]{4,2,0,3,1:T(2,128)}), f32[8,4,2,16,512]{4,2,0,3,1:T(2,128)S(1)}, u32[]{:S(2)}, u32[]{:S(2)}) async-start(f32[8,4,2,16,512]{4,2,0,3,1:T(2,128)} %copy.19), calls=%async_computation | async-start | bytes 4194304 | tf_op jit(solution)/shard_map/all_to_all | solution.py:38
  16.5 0.0 copy-done
  16.5 0.0 copy-done.1
  16.5 0.0 copy-done.2
  16.5 0.0 copy-done.3
  16.5 4.6 %multiply_add_fusion = f32[64,32,1024]{2,1,0:T(8,128)} fusion(f32[32,1024]{1,0:T(8,128)S(1)} %copy-done.2, f32[64,1024]{1,0:T(8,128)S(1)} %copy-done, f32[32,1024]{1,0:T(8,128)S(1)} %copy-done.3, f32[64,1024]{1,0:T(8,128)S(1)} %copy-done.1), kind=kLoop, calls=%fused_computation | loop fusion | flops 6291456 | bytes 9175040 | tf_op jit(solution)/shard_map/add | solution.py:28
  21.1 21.0 %all-to-all-done = f32[8,4,2,16,512]{4,2,0,3,1:T(2,128)S(1)} async-done(((f32[8,4,2,16,512]{4,2,0,3,1:T(2,128)}), f32[8,4,2,16,512]{4,2,0,3,1:T(2,128)S(1)}, u32[]{:S(2)}, u32[]{:S(2)}) %all-to-all-start) | async-done | bytes 2097184 | tf_op jit(solution)/shard_map/all_to_all | solution.py:38
  42.2 2.7 %copy.20 = f32[8,1,2,16,4,512]{5,4,3,2,0,1:T(4,128)} copy(f32[8,1,2,16,4,512]{5,2,0,3,4,1:T(2,128)S(1)} %bitcast.30) | data formatting | bytes 4194304 | tf_op jit(solution)/shard_map/all_to_all | solution.py:38
  44.9 2.7 %reshape.70 = f32[8,2,16,2048]{3,2,1,0:T(8,128)S(1)} reshape(f32[8,1,2,16,4,512]{5,4,3,2,0,1:T(4,128)} %copy.20) | data formatting | bytes 4194304 | tf_op jit(solution)/shard_map/reshape | solution.py:39
  47.6 6.5 %fusion.2 = f32[8,2,16,1024]{3,2,1,0:T(8,128)S(1)} fusion(f32[8,2,16,2048]{3,2,1,0:T(8,128)S(1)} %reshape.70, f32[2048,1024,1,1]{1,0,3,2:T(8,128)} %bitcast.29), kind=kOutput, calls=%fused_computation.6 | convolution fusion | flops 3221225472 | bytes 11534336 | tf_op jit(solution)/shard_map/neyz,zk->neyk/dot_general | solution.py:40
  54.0 0.0 copy-start.4
  54.1 0.0 copy-start.5
  54.1 0.0 copy-start.6
  54.1 0.0 slice-start
  54.1 32.0 %all_to_all.48 = f32[8,2,16,1024]{3,2,1,0:T(8,128)S(1)} all-to-all(f32[8,2,16,1024]{3,2,1,0:T(8,128)S(1)} %fusion.2), channel_id=1, replica_groups=mesh['north'=8,'deep'=4] {'north'}, dimensions={0} | all-to-all | bytes 2097152 | tf_op jit(solution)/shard_map/all_to_all | solution.py:41
  86.1 0.1 copy.21
  86.2 0.0 copy-done.4
  86.2 0.4 convolution_bitcast_fusion
  86.7 1.2 %copy.22 = f32[2,64,1024]{2,0,1:T(2,128)} copy(f32[2,64,1024]{2,1,0:T(8,128)S(1)} %convolution_bitcast_fusion) | data formatting | bytes 1048576 | tf_op jit(solution)/shard_map/eyz,yk->ekz/transpose | solution.py:43
  87.9 3.5 %all-to-all-start.2 = ((f32[2,64,1024]{2,0,1:T(2,128)}), f32[2,64,1024]{2,0,1:T(2,128)S(1)}, u32[]{:S(2)}, u32[]{:S(2)}) async-start(f32[2,64,1024]{2,0,1:T(2,128)} %copy.22), calls=%async_computation.2 | async-start | bytes 1048576 | tf_op jit(solution)/shard_map/all_to_all | solution.py:44
  91.4 0.0 copy-done.5
  91.4 0.1 dynamic_slice.7
  91.5 0.0 copy-done.6
  91.5 0.1 dynamic_slice.6
  91.5 0.1 broadcast_add_fusion
  91.6 8.5 %all-to-all-done.2 = f32[2,64,1024]{2,0,1:T(2,128)S(1)} async-done(((f32[2,64,1024]{2,0,1:T(2,128)}), f32[2,64,1024]{2,0,1:T(2,128)S(1)}, u32[]{:S(2)}, u32[]{:S(2)}) %all-to-all-start.2) | async-done | bytes 524320 | tf_op jit(solution)/shard_map/all_to_all | solution.py:44
  100.1 0.2 copy.23
  100.3 0.0 slice-done
  100.3 0.9 bitcast_multiply_fusion
Async XLA Ops:
  7.9 8.5 %copy-start = (f32[64,1024]{1,0:T(8,128)S(1)}, f32[64,1024]{1,0:T(8,128)}, u32[]{:S(2)}) copy-start(f32[64,1024]{1,0:T(8,128)} %constant.29.clone) | copy-start | bytes 786436
  7.9 8.5 %copy-start.1 = (f32[64,1024]{1,0:T(8,128)S(1)}, f32[64,1024]{1,0:T(8,128)}, u32[]{:S(2)}) copy-start(f32[64,1024]{1,0:T(8,128)} %constant.28.clone) | copy-start | bytes 786436
  7.9 8.5 %copy-start.2 = (f32[32,1024]{1,0:T(8,128)S(1)}, f32[32,1024]{1,0:T(8,128)}, u32[]{:S(2)}) copy-start(f32[32,1024]{1,0:T(8,128)} %constant.30.clone) | copy-start | bytes 393220
  7.9 8.6 %copy-start.3 = (f32[32,1024]{1,0:T(8,128)S(1)}, f32[32,1024]{1,0:T(8,128)}, u32[]{:S(2)}) copy-start(f32[32,1024]{1,0:T(8,128)} %constant.31.clone) | copy-start | bytes 393220
  12.2 29.9 %all-to-all-start = ((f32[8,4,2,16,512]{4,2,0,3,1:T(2,128)}), f32[8,4,2,16,512]{4,2,0,3,1:T(2,128)S(1)}, u32[]{:S(2)}, u32[]{:S(2)}) async-start(f32[8,4,2,16,512]{4,2,0,3,1:T(2,128)} %copy.19), calls=%async_computation | async-start | bytes 4194304 | tf_op jit(solution)/shard_map/all_to_all | solution.py:38
  54.0 32.2 %copy-start.4 = (f32[128,64,1]{0,1,2:T(8,128)S(1)}, f32[128,64,1]{0,1,2:T(8,128)}, u32[]{:S(2)}) copy-start(f32[128,64,1]{0,1,2:T(8,128)} %constant.32) | copy-start | bytes 98308
  54.1 37.3 %copy-start.5 = (f32[128]{0:T(128)S(1)}, f32[128]{0:T(128)}, u32[]{:S(2)}) copy-start(f32[128]{0:T(128)} %param.12) | copy-start | bytes 1540
  54.1 37.4 %copy-start.6 = (f32[128]{0:T(128)S(1)}, f32[128]{0:T(128)}, u32[]{:S(2)}) copy-start(f32[128]{0:T(128)} %param.11) | copy-start | bytes 1540
  54.1 46.2 %slice-start = ((f32[2048]{0:T(1024)}), f32[1024]{0:T(1024)S(1)}, s32[]{:S(2)}) async-start(f32[2048]{0:T(1024)} %param.13), calls=%async_computation.3 | async-start | bytes 8192 | tf_op jit(solution)/shard_map/slice | solution.py:47
  87.9 12.3 %all-to-all-start.2 = ((f32[2,64,1024]{2,0,1:T(2,128)}), f32[2,64,1024]{2,0,1:T(2,128)S(1)}, u32[]{:S(2)}, u32[]{:S(2)}) async-start(f32[2,64,1024]{2,0,1:T(2,128)} %copy.22), calls=%async_computation.2 | async-start | bytes 1048576 | tf_op jit(solution)/shard_map/all_to_all | solution.py:44

commit v2 on v1

v2 whole, which is shorter than its diff:
```python
import functools

import jax
import jax.numpy as jnp
import numpy as np
from jax import lax
from jax.experimental import pallas as pl
from jax.experimental.pallas import tpu as pltpu
from jax.sharding import PartitionSpec as P

F32, BF16 = jnp.float32, jnp.bfloat16
FINE = 32
TILE = 256


def angles(rows, modes, count):
    rank = np.outer(rows, modes) % (2 * count + 2)
    return np.pi / (count + 1) * rank


def split_np(table):
    high = table.astype(np.float32).astype(BF16)
    low = (table - high.astype(np.float64)).astype(np.float32).astype(BF16)
    return high, low


def left_table(count):
    gain = (2.0 / (count + 1)) ** 0.5
    table = np.sin(angles(np.arange(1, count // 2 + 1), np.arange(1, count + 1), count)) * gain
    return split_np(table)


def stacked(high, low):
    return jnp.asarray(np.block([[high, high], [low, np.zeros_like(low)]]))


def long_tables(count):
    modes = np.arange(1, count // 2 + 1)
    gain = (2.0 / (count + 1)) ** 0.5
    coarse = angles(np.arange(0, count, FINE), modes, count)
    step = angles(np.arange(1, FINE + 1), modes, count)
    f32 = lambda v: jnp.asarray(v.astype(np.float32))
    return f32(np.sin(coarse) * gain), f32(np.cos(coarse) * gain), f32(np.sin(step)), f32(np.cos(step))


def split(values):
    high = values.astype(BF16)
    return high, (values - high.astype(F32)).astype(BF16)


def dot(a, b):
    return jnp.dot(a, b, preferred_element_type=F32)


def kernel(
    north, deep, each,
    src, tx, ty, sin_a, cos_a, sin_b, cos_b,
    out,
    send1, recv1, send2, recv2, send3, recv3, t_high, t_low, left, acc,
    s1, r1, s2, r2, s3, r3,
):
    me_n, me_d = lax.axis_index("north"), lax.axis_index("deep")
    ny_part, nx, nz_part = src.shape
    kept_x = nx // 2
    kept_z = t_high.shape[1]
    rows = ny_part * north

    barrier = pltpu.get_barrier_semaphore()
    for r in range(1, deep):
        pl.semaphore_signal(barrier, inc=1, device_id={"deep": lax.rem(me_d + r, deep)})
    for r in range(1, north):
        pl.semaphore_signal(barrier, inc=1, device_id={"north": lax.rem(me_n + r, north)})

    def x_step(y, carry):
        high, low = split(src[y])
        both = dot(tx[...], jnp.concatenate([high, low], axis=0))
        modes = both[:kept_x] + both[kept_x:]
        at = pl.multiple_of(y * north, north)
        for e in range(each):
            for d in range(deep):
                first = (e * deep + d) * north
                send1[e, d, pl.ds(at, north), :] = modes[first : first + north]
        return carry

    lax.fori_loop(0, ny_part, x_step, 0)
    pl.semaphore_wait(barrier, deep + north - 2)

    copies1 = {}
    for e in range(each):
        for r in range(1, deep):
            to = lax.rem(me_d + r, deep)
            copies1[e, r] = pltpu.make_async_remote_copy(
                src_ref=send1.at[e, to],
                dst_ref=recv1.at[e, me_d],
                send_sem=s1.at[e, r],
                recv_sem=r1.at[e, r],
                device_id={"deep": to},
            )
            copies1[e, r].start()

    def table_step(a, carry):
        table = sin_a[pl.ds(a, 1), :] * cos_b[...] + cos_a[pl.ds(a, 1), :] * sin_b[...]
        high, low = split(table)
        at = pl.multiple_of(a * FINE, FINE)
        t_high[pl.ds(at, FINE), :] = high
        t_low[pl.ds(at, FINE), :] = low
        return carry

    lax.fori_loop(0, sin_a.shape[0], table_step, 0)

    def z_product(values, owner, first):
        high, low = split(values)
        left[:rows, :] = high
        left[rows:, :] = low
        at = pl.multiple_of(owner * nz_part, nz_part)

        def z_step(t, carry):
            cols = pl.ds(pl.multiple_of(t * TILE, TILE), TILE)
            both = dot(left[...], t_high[pl.ds(at, nz_part), cols])
            total = both[:rows] + both[rows:] + dot(left[:rows, :], t_low[pl.ds(at, nz_part), cols])
            if first:
                acc[:, cols] = total
            else:
                acc[:, cols] += total
            return carry

        lax.fori_loop(0, kept_z // TILE, z_step, 0)

    copies2 = {}
    for e in range(each):
        z_product(send1[e, me_d], me_d, True)
        for r in range(1, deep):
            copies1[e, r].wait_recv()
            owner = lax.rem(me_d - r + deep, deep)
            z_product(recv1[e, owner], owner, False)
        for c in range(0, kept_z, TILE):
            part = acc[:, c : c + TILE].reshape(ny_part, north, TILE)
            send2[e, :, :, c : c + TILE] = jnp.swapaxes(part, 0, 1)
        recv2[e, me_n] = send2[e, me_n]
        for r in range(1, north):
            to = lax.rem(me_n + r, north)
            copies2[e, r] = pltpu.make_async_remote_copy(
                src_ref=send2.at[e, to],
                dst_ref=recv2.at[e, me_n],
                send_sem=s2.at[e, r],
                recv_sem=r2.at[e, r],
                device_id={"north": to},
            )
            copies2[e, r].start()

    copies3 = {}
    kept_y = ny_part * north // 2
    share_y = kept_y // deep
    for e in range(each):
        for r in range(1, north):
            copies2[e, r].wait_recv()
        for c in range(0, kept_z, TILE):
            values = recv2[e, :, :, c : c + TILE].reshape(rows, TILE)
            both = dot(ty[...], jnp.concatenate(split(values), axis=0))
            modes = both[:kept_y] + both[kept_y:]
            send3[e, :, :, c : c + TILE] = modes.reshape(deep, share_y, TILE)
        recv3[me_d, e] = send3[e, me_d]
        for r in range(1, deep):
            to = lax.rem(me_d + r, deep)
            copies3[e, r] = pltpu.make_async_remote_copy(
                src_ref=send3.at[e, to],
                dst_ref=recv3.at[me_d, e],
                send_sem=s3.at[e, r],
                recv_sem=r3.at[e, r],
                device_id={"deep": to},
            )
            copies3[e, r].start()

    for copies in (copies1, copies2):
        for copy in copies.values():
            copy.wait_send()
    for copy in copies3.values():
        copy.wait()
    out[...] = recv3[...]


def on_device(source, symbol_x, symbol_y, symbol_z):
    north, deep = lax.axis_size("north"), lax.axis_size("deep")
    nx, ny_part, nz_part = source.shape
    each = nx // 2 // north // deep
    ny, nz = ny_part * north, nz_part * deep
    kept_z, share_y = nz // 2, ny // 2 // deep
    order = np.arange(nx // 2).reshape(north, deep, each).transpose(2, 1, 0).reshape(-1)
    x_high, x_low = left_table(nx)
    tx = stacked(x_high[order], x_low[order])
    ty = stacked(*left_table(ny))
    rows = ny_part * north
    vmem = pl.BlockSpec(memory_space=pltpu.VMEM)
    v = pl.pallas_call(
        functools.partial(kernel, north, deep, each),
        out_shape=jax.ShapeDtypeStruct((deep, each, share_y, kept_z), F32),
        in_specs=[vmem] * 7,
        out_specs=vmem,
        scratch_shapes=[
            pltpu.VMEM((each, deep, rows, nz_part), F32),
            pltpu.VMEM((each, deep, rows, nz_part), F32),
            pltpu.VMEM((each, north, ny_part, kept_z), F32),
            pltpu.VMEM((each, north, ny_part, kept_z), F32),
            pltpu.VMEM((each, deep, share_y, kept_z), F32),
            pltpu.VMEM((deep, each, share_y, kept_z), F32),
            pltpu.VMEM((nz, kept_z), BF16),
            pltpu.VMEM((nz, kept_z), BF16),
            pltpu.VMEM((2 * rows, nz_part), BF16),
            pltpu.VMEM((rows, kept_z), F32),
        ]
        + [pltpu.SemaphoreType.DMA((each, n)) for n in (deep, deep, north, north, deep, deep)],
        compiler_params=pltpu.CompilerParams(
            collective_id=0, has_side_effects=True, vmem_limit_bytes=67043328
        ),
    )(jnp.swapaxes(source, 0, 1), tx, ty, *long_tables(nz))
    v = v.reshape(deep * each, share_y, kept_z)
    part_x = lax.dynamic_slice_in_dim(symbol_x, lax.axis_index("north") * v.shape[0], v.shape[0])
    part_y = lax.dynamic_slice_in_dim(symbol_y, lax.axis_index("deep") * v.shape[1], v.shape[1])
    symbol = part_x[:, None, None] + part_y[None, :, None] + symbol_z[: v.shape[2]][None, None, :]
    return v * lax.rsqrt(symbol)


def solution(mesh):
    in_specs = (P(None, "north", "deep"), P(), P(), P())
    out_specs = P("north", "deep", None)
    return jax.shard_map(
        on_device, mesh=mesh, in_specs=in_specs, out_specs=out_specs, check_vma=False
    )
```

time: 102 us -> 58.8 us (0.58)
  the two profiles are of different devices: /device:TPU:0 before, /device:TPU:15 now
where the time goes in v2:
time: 58.8 us; the launch traced here: 58.6 us
  Pallas kernels  47.8 us (81%)
  local copies, waits for them, and re-layouts  8.69 us (15%)
  other arithmetic  2.05 us (3%)
    pallas_call x1, Pallas kernels, on_device(): pl.pallas_call(functools.partial(kernel, north, deep, each), out_shape=ja...  47.8 us
    unnamed x1, local copies, waits for them, and re-layouts  6.54 us
    mul x1, other arithmetic, on_device(): return v * lax.rsqrt(symbol)  1.98 us

profile of v2, /device:TPU:15, one launch (start us, length us, event | category | flops | bytes accessed | tf_op | source)
XLA Modules:
  0.0 58.6 jit_solution(15628507900865993940)
XLA Ops:
  0.0 6.5 %copy.13 = f32[128,16,512]{2,0,1:T(8,128)} copy(f32[128,16,512]{2,1,0:T(8,128)} %param.10) | data formatting | bytes 8388608 | tf_op args[0]
  6.5 47.8 %shard_map.100 = f32[4,2,16,1024]{3,2,1,0:T(8,128)} custom-call(f32[16,128,512]{2,1,0:T(8,128)} %bitcast.5, bf16[128,256]{1,0:T(8,128)(2,1)} %constant.29.clone.tx, bf16[128,256]{1,0:T(8,128)(2,1)} %constant.30.clone.ty, f32[64,1024]{1,0:T(8,128)} %constant.31.clone.sin_a, f32[64,1024]{1,0:T(8,128)} %constant.32.clone.cos_a, ...), custom_call_target="tpu_custom_call" | custom-call | tf_op jit(solution)/shard_map/pallas_call | solution.py:194
  54.4 0.7 %slice.3 = f32[1024]{0:T(1024)S(1)} slice(f32[2048]{0:T(1024)} %param.13), slice={[0:1024]} | slice | bytes 8192 | tf_op jit(solution)/shard_map/slice | solution.py:219
  55.1 0.7 %dynamic_slice.7 = f32[16]{0:T(128)S(1)} dynamic-slice(f32[128]{0:T(128)} %param.12, s32[]{:T(128)S(6)} %select_n.7), dynamic_slice_sizes={16} | dynamic-slice | bytes 132 | tf_op jit(solution)/shard_map/dynamic_slice | solution.py:218
  55.8 0.7 %dynamic_slice.6 = f32[8]{0:T(128)S(1)} dynamic-slice(f32[128]{0:T(128)} %param.11, s32[]{:T(128)S(6)} %select_n.6), dynamic_slice_sizes={8} | dynamic-slice | bytes 68 | tf_op jit(solution)/shard_map/dynamic_slice | solution.py:217
  56.5 0.1 broadcast_add_fusion
  56.6 2.0 %bitcast_multiply_fusion = f32[8,16,1024]{2,1,0:T(8,128)} fusion(f32[4,2,16,1024]{3,2,1,0:T(8,128)} %shard_map.100, f32[1024]{0:T(1024)S(1)} %slice.3, f32[8,16]{1,0:T(8,128)S(1)} %broadcast_add_fusion), kind=kLoop, calls=%fused_computation.1 | loop fusion | flops 262144 | bytes 1053184 | tf_op jit(solution)/shard_map/mul | solution.py:220

commit v3 on v2

v3 whole, which is shorter than its diff:
```python
import functools

import jax
import jax.numpy as jnp
import numpy as np
from jax import lax
from jax.experimental import pallas as pl
from jax.experimental.pallas import tpu as pltpu
from jax.sharding import PartitionSpec as P

F32, BF16 = jnp.float32, jnp.bfloat16
FINE = 32
TILE = 256
SUB = 8


def angles(rows, modes, count):
    rank = np.outer(rows, modes) % (2 * count + 2)
    return np.pi / (count + 1) * rank


def split_np(table):
    high = table.astype(np.float32).astype(BF16)
    low = (table - high.astype(np.float64)).astype(np.float32).astype(BF16)
    return high, low


def left_table(count):
    gain = (2.0 / (count + 1)) ** 0.5
    table = np.sin(angles(np.arange(1, count // 2 + 1), np.arange(1, count + 1), count)) * gain
    return split_np(table)


def stacked(high, low):
    return jnp.asarray(np.block([[high, high], [low, np.zeros_like(low)]]))


def long_tables(count):
    modes = np.arange(1, count // 2 + 1)
    gain = (2.0 / (count + 1)) ** 0.5
    coarse = angles(np.arange(0, count, FINE), modes, count)
    step = angles(np.arange(1, FINE + 1), modes, count)
    f32 = lambda v: jnp.asarray(v.astype(np.float32))
    return f32(np.sin(coarse) * gain), f32(np.cos(coarse) * gain), f32(np.sin(step)), f32(np.cos(step))


def split(values):
    high = values.astype(BF16)
    return high, (values - high.astype(F32)).astype(BF16)


def dot(a, b):
    return jnp.dot(a, b, preferred_element_type=F32)


def kernel(
    north, deep, each,
    src, tx, ty, sin_a, cos_a, sin_b, cos_b, symbol_x, symbol_y, symbol_z,
    out,
    turned, send1, recv1, send2, recv2, send3, recv3, t_high, t_low, left, acc,
    s1, r1, s2, r2, s3, r3,
):
    me_n, me_d = lax.axis_index("north"), lax.axis_index("deep")
    nx, ny_part, nz_part = src.shape
    halves = ny_part // SUB
    kept_x = nx // 2
    kept_z = t_high.shape[1]
    rows = SUB * north
    kept_y = ny_part * north // 2
    share_y = kept_y // deep

    barrier = pltpu.get_barrier_semaphore()
    for r in range(1, deep):
        pl.semaphore_signal(barrier, inc=1, device_id={"deep": lax.rem(me_d + r, deep)})
    for r in range(1, north):
        pl.semaphore_signal(barrier, inc=1, device_id={"north": lax.rem(me_n + r, north)})

    def x_product(h):
        for c in range(0, nz_part, TILE):

            def turn(g, carry):
                at = pl.multiple_of(g * 16, 16)
                part = src[pl.ds(at, 16), h * SUB : (h + 1) * SUB, c : c + TILE]
                high, low = split(jnp.swapaxes(part, 0, 1))
                turned[:, pl.ds(at, 16), :] = high
                turned[:, pl.ds(pl.multiple_of(nx + at, 16), 16), :] = low
                return carry

            lax.fori_loop(0, nx // 16, turn, 0)

            def x_step(y, carry):
                both = dot(tx[...], turned[y])
                modes = both[:kept_x] + both[kept_x:]
                at = pl.multiple_of(y * north, north)
                for e in range(each):
                    for d in range(deep):
                        first = (e * deep + d) * north
                        send1[e, h, d, pl.ds(at, north), c : c + TILE] = modes[first : first + north]
                return carry

            lax.fori_loop(0, SUB, x_step, 0)

    copies1 = {}

    def send_modes(e, h):
        for r in range(1, deep):
            to = lax.rem(me_d + r, deep)
            copies1[e, h, r] = pltpu.make_async_remote_copy(
                src_ref=send1.at[e, h, to],
                dst_ref=recv1.at[e, h, me_d],
                send_sem=s1.at[e * halves + h, r],
                recv_sem=r1.at[e * halves + h, r],
                device_id={"deep": to},
            )
            copies1[e, h, r].start()

    for h in range(halves):
        x_product(h)
        if h == 0:
            pl.semaphore_wait(barrier, deep + north - 2)
        send_modes(0, h)
    for e in range(1, each):
        for h in range(halves):
            send_modes(e, h)

    def table_step(a, carry):
        table = sin_a[pl.ds(a, 1), :] * cos_b[...] + cos_a[pl.ds(a, 1), :] * sin_b[...]
        high, low = split(table)
        at = pl.multiple_of(a * FINE, FINE)
        t_high[pl.ds(at, FINE), :] = high
        t_low[pl.ds(at, FINE), :] = low
        return carry

    lax.fori_loop(0, sin_a.shape[0], table_step, 0)

    def inverse_roots():
        row = lax.broadcasted_iota(jnp.int32, (share_y, TILE), 0)
        part_y = jnp.zeros((share_y, TILE), F32)
        for j in range(share_y):
            part_y = jnp.where(row == j, symbol_y[me_d * share_y + j], part_y)
        for d in range(deep):
            for e in range(each):
                part_x = symbol_x[me_n * deep * each + d * each + e]
                for c in range(0, kept_z, TILE):
                    out[d, e, :, c : c + TILE] = lax.rsqrt(part_x + part_y + symbol_z[:, c : c + TILE])

    inverse_roots()

    def z_product(values, owner, first):
        high, low = split(values)
        left[:rows, :] = high
        left[rows:, :] = low
        at = pl.multiple_of(owner * nz_part, nz_part)

        def z_step(t, carry):
            cols = pl.ds(pl.multiple_of(t * TILE, TILE), TILE)
            both = dot(left[...], t_high[pl.ds(at, nz_part), cols])
            total = both[:rows] + both[rows:] + dot(left[:rows, :], t_low[pl.ds(at, nz_part), cols])
            if first:
                acc[:, cols] = total
            else:
                acc[:, cols] += total
            return carry

        lax.fori_loop(0, kept_z // TILE, z_step, 0)

    copies2 = {}
    for e in range(each):
        for h in range(halves):
            z_product(send1[e, h, me_d], me_d, True)
            for r in range(1, deep):
                copies1[e, h, r].wait_recv()
                owner = lax.rem(me_d - r + deep, deep)
                z_product(recv1[e, h, owner], owner, False)
            for c in range(0, kept_z, TILE):
                part = acc[:, c : c + TILE].reshape(SUB, north, TILE)
                send2[e, h, :, :, c : c + TILE] = jnp.swapaxes(part, 0, 1)
            recv2[e, h, me_n] = send2[e, h, me_n]
            for r in range(1, north):
                to = lax.rem(me_n + r, north)
                copies2[e, h, r] = pltpu.make_async_remote_copy(
                    src_ref=send2.at[e, h, to],
                    dst_ref=recv2.at[e, h, me_n],
                    send_sem=s2.at[e * halves + h, r],
                    recv_sem=r2.at[e * halves + h, r],
                    device_id={"north": to},
                )
                copies2[e, h, r].start()

    copies3 = {}
    for e in range(each):
        for h in range(halves):
            for r in range(1, north):
                copies2[e, h, r].wait_recv()
        for c in range(0, kept_z, TILE):
            values = recv2[e, :, :, :, c : c + TILE].reshape(ny_part * north, TILE)
            both = dot(ty[...], jnp.concatenate(split(values), axis=0))
            modes = both[:kept_y] + both[kept_y:]
            send3[e, :, :, c : c + TILE] = modes.reshape(deep, share_y, TILE)
        recv3[me_d, e] = send3[e, me_d]
        for r in range(1, deep):
            to = lax.rem(me_d + r, deep)
            copies3[e, r] = pltpu.make_async_remote_copy(
                src_ref=send3.at[e, to],
                dst_ref=recv3.at[me_d, e],
                send_sem=s3.at[e, r],
                recv_sem=r3.at[e, r],
                device_id={"deep": to},
            )
            copies3[e, r].start()

    for copies in (copies1, copies2):
        for copy in copies.values():
            copy.wait_send()
    for copy in copies3.values():
        copy.wait()
    out[...] = out[...] * recv3[...]


def on_device(source, symbol_x, symbol_y, symbol_z):
    north, deep = lax.axis_size("north"), lax.axis_size("deep")
    nx, ny_part, nz_part = source.shape
    each, halves = nx // 2 // north // deep, ny_part // SUB
    ny, nz = ny_part * north, nz_part * deep
    kept_z, share_y = nz // 2, ny // 2 // deep
    order = np.arange(nx // 2).reshape(north, deep, each).transpose(2, 1, 0).reshape(-1)
    x_high, x_low = left_table(nx)
    tx = stacked(x_high[order], x_low[order])
    order = np.arange(ny).reshape(north, halves, SUB).transpose(1, 0, 2).reshape(-1)
    y_high, y_low = left_table(ny)
    ty = stacked(y_high[:, order], y_low[:, order])
    rows = SUB * north
    vmem = pl.BlockSpec(memory_space=pltpu.VMEM)
    smem = pl.BlockSpec(memory_space=pltpu.SMEM)
    chunks = each * halves
    v = pl.pallas_call(
        functools.partial(kernel, north, deep, each),
        out_shape=jax.ShapeDtypeStruct((deep, each, share_y, kept_z), F32),
        in_specs=[vmem] * 7 + [smem] * 2 + [vmem],
        out_specs=vmem,
        scratch_shapes=[
            pltpu.VMEM((SUB, 2 * nx, TILE), BF16),
            pltpu.VMEM((each, halves, deep, rows, nz_part), F32),
            pltpu.VMEM((each, halves, deep, rows, nz_part), F32),
            pltpu.VMEM((each, halves, north, SUB, kept_z), F32),
            pltpu.VMEM((each, halves, north, SUB, kept_z), F32),
            pltpu.VMEM((each, deep, share_y, kept_z), F32),
            pltpu.VMEM((deep, each, share_y, kept_z), F32),
            pltpu.VMEM((nz, kept_z), BF16),
            pltpu.VMEM((nz, kept_z), BF16),
            pltpu.VMEM((2 * rows, nz_part), BF16),
            pltpu.VMEM((rows, kept_z), F32),
        ]
        + [
            pltpu.SemaphoreType.DMA((sets, peers))
            for sets, peers in ((chunks, deep), (chunks, north), (each, deep))
            for _ in range(2)
        ],
        compiler_params=pltpu.CompilerParams(
            collective_id=0, has_side_effects=True, vmem_limit_bytes=67043328
        ),
    )(source, tx, ty, *long_tables(nz), symbol_x, symbol_y, symbol_z[None, :])
    return v.reshape(deep * each, share_y, kept_z)


def solution(mesh):
    in_specs = (P(None, "north", "deep"), P(), P(), P())
    out_specs = P("north", "deep", None)
    return jax.shard_map(
        on_device, mesh=mesh, in_specs=in_specs, out_specs=out_specs, check_vma=False
    )
```

time: 58.8 us -> 50.3 us (0.86)
  the two profiles are of different devices: /device:TPU:15 before, /device:TPU:0 now
where the time goes in v3:
time: 50.3 us; the launch traced here: 50.1 us
  Pallas kernels  48.2 us (96%)
  local copies, waits for them, and re-layouts  1.89 us (4%)
    pallas_call x1, Pallas kernels, on_device(): pl.pallas_call(functools.partial(kernel, north, deep, each), out_shape=ja...  48.2 us
    unnamed x1, local copies, waits for them, and re-layouts  1.89 us

profile of v3, /device:TPU:0, one launch (start us, length us, event | category | flops | bytes accessed | tf_op | source)
XLA Modules:
  0.0 50.1 jit_solution(12272352580439204410)
XLA Ops:
  0.0 48.2 %shard_map.100 = f32[4,2,16,1024]{3,2,1,0:T(8,128)} custom-call(f32[128,16,512]{2,1,0:T(8,128)} %src.1, bf16[128,256]{1,0:T(8,128)(2,1)} %constant.12.clone.tx, bf16[128,256]{1,0:T(8,128)(2,1)} %constant.13.clone.ty, f32[64,1024]{1,0:T(8,128)} %constant.14.clone.sin_a, f32[64,1024]{1,0:T(8,128)} %constant.15.clone.cos_a, f32[32,1024]{1,0:T(8,128)} %constant.16.clone.sin_b, ...), custom_call_target="tpu_custom_call" | custom-call | tf_op jit(solution)/shard_map/pallas_call | solution.py:236
  48.3 1.9 %copy.12 = f32[8,16,1024]{2,1,0:T(8,128)} copy(f32[8,16,1024]{2,1,0:T(8,128)} %bitcast.2) | data formatting | bytes 1048576

commit v4 on v3

--- a/solution.py
+++ b/solution.py
@@ -55,10 +55,10 @@
 
 def kernel(
     north, deep, each,
-    src, tx, ty, sin_a, cos_a, sin_b, cos_b, symbol_x, symbol_y, symbol_z,
+    source, tx, ty, sin_a, cos_a, sin_b, cos_b, symbol_x, symbol_y, symbol_z,
     out,
-    turned, send1, recv1, send2, recv2, send3, recv3, t_high, t_low, left, acc,
-    s1, r1, s2, r2, s3, r3,
+    src, turned, send1, recv1, send2, recv2, send3, recv3, t_high, t_low, left, acc,
+    s1, r1, s2, r2, s3, r3, loaded,
 ):
     me_n, me_d = lax.axis_index("north"), lax.axis_index("deep")
     nx, ny_part, nz_part = src.shape
@@ -68,6 +68,12 @@
     rows = SUB * north
     kept_y = ny_part * north // 2
     share_y = kept_y // deep
+
+    loads = []
+    for h in range(halves):
+        planes = (slice(None), pl.ds(h * SUB, SUB))
+        loads.append(pltpu.make_async_copy(source.at[planes], src.at[planes], loaded.at[h]))
+        loads[h].start()
 
     barrier = pltpu.get_barrier_semaphore()
     for r in range(1, deep):
@@ -115,6 +121,7 @@
             copies1[e, h, r].start()
 
     for h in range(halves):
+        loads[h].wait()
         x_product(h)
         if h == 0:
             pl.semaphore_wait(barrier, deep + north - 2)
@@ -236,9 +243,10 @@
     v = pl.pallas_call(
         functools.partial(kernel, north, deep, each),
         out_shape=jax.ShapeDtypeStruct((deep, each, share_y, kept_z), F32),
-        in_specs=[vmem] * 7 + [smem] * 2 + [vmem],
+        in_specs=[pl.BlockSpec(memory_space=pl.ANY)] + [vmem] * 6 + [smem] * 2 + [vmem],
         out_specs=vmem,
         scratch_shapes=[
+            pltpu.VMEM(source.shape, F32),
             pltpu.VMEM((SUB, 2 * nx, TILE), BF16),
             pltpu.VMEM((each, halves, deep, rows, nz_part), F32),
             pltpu.VMEM((each, halves, deep, rows, nz_part), F32),
@@ -255,7 +263,8 @@
             pltpu.SemaphoreType.DMA((sets, peers))
             for sets, peers in ((chunks, deep), (chunks, north), (each, deep))
             for _ in range(2)
-        ],
+        ]
+        + [pltpu.SemaphoreType.DMA((halves,))],
         compiler_params=pltpu.CompilerParams(
             collective_id=0, has_side_effects=True, vmem_limit_bytes=67043328
         ),

time: 50.3 us -> 50.6 us (level)
  no operation moved by 1% of the time
where the time goes in v4:
time: 50.6 us; the launch traced here: 50.4 us
  Pallas kernels  48.5 us (96%)
  local copies, waits for them, and re-layouts  1.89 us (4%)
    pallas_call x1, Pallas kernels, on_device(): pl.pallas_call(functools.partial(kernel, north, deep, each), out_shape=ja...  48.5 us
    unnamed x1, local copies, waits for them, and re-layouts  1.89 us

profile of v4, /device:TPU:0, one launch (start us, length us, event | category | flops | bytes accessed | tf_op | source)
XLA Modules:
  0.0 50.4 jit_solution(14558812020220606310)
XLA Ops:
  0.0 48.5 %shard_map.100 = f32[4,2,16,1024]{3,2,1,0:T(8,128)} custom-call(f32[128,16,512]{2,1,0:T(8,128)} %source.1, bf16[128,256]{1,0:T(8,128)(2,1)} %constant.12.clone.tx, bf16[128,256]{1,0:T(8,128)(2,1)} %constant.13.clone.ty, f32[64,1024]{1,0:T(8,128)} %constant.14.clone.sin_a, f32[64,1024]{1,0:T(8,128)} %constant.15.clone.cos_a, ...), custom_call_target="tpu_custom_call" | custom-call | tf_op jit(solution)/shard_map/pallas_call | solution.py:243
  48.5 1.9 %copy.12 = f32[8,16,1024]{2,1,0:T(8,128)} copy(f32[8,16,1024]{2,1,0:T(8,128)} %bitcast.2) | data formatting | bytes 1048576
